TPU v7x, 128 devices: a whole 4x4x4 slice. The times are simulated.
128 devices in a mesh: layer: 4 (over z_hi, core), grid: 32 (over y, x, z_lo).
Axes of the slice: x: 4, y: 4, z: 4 (z_hi: 2, z_lo: 2; z = z_hi * 2 + z_lo), core: 2. Of those that a mesh axis runs over, the one named last changes fastest.
Arguments:
- fourier: float32 [1024, 512, 256], P(('layer', 'grid')), may hold values from -6 to 6
- weights: float32 [1024], P(('layer', 'grid')), may hold values from 0.009375 to 0.09375
- legendre: float32 [256, 513, 1024], P('grid'), may hold values from -6 to 6
- pair_slots: int32 [256], replicated, may hold values from 0 to 255, each once
Outputs:
- spectra: float32 [256, 513, 256], P('grid', None, 'layer')
Inputs may be any that keep to these rules, and one draw needn't show every extreme that they name: Each pair index appears exactly once; position q holds wavenumbers pair_slots[q] and 511 - pair_slots[q].
All inputs are finite; a program needn't handle non-finite values.
Results may differ from a plain program's by a relative error of at most 0.0003.
Values sent between devices are 32-bit elements; how exact they have to be, the bound alone decides.
No kernel may reach another device: no remote copies, remote signals or barrier semaphores. Data moves between devices by JAX's collectives and lax.ppermute only.
A program may use at most 128 MiB of HBM per device.

v0:
```python
import jax
import jax.numpy as jnp
from jax import lax
from jax.sharding import PartitionSpec as P


def project(poly_block, values, limits):
    local_pairs = poly_block.shape[0]
    slots_view = values.reshape(values.shape[0], local_pairs, 2, values.shape[2])
    product = jnp.einsum(
        "qrl,lqsc->qrsc",
        poly_block,
        slots_view,
        precision=lax.Precision.HIGHEST,
        preferred_element_type=jnp.float32,
    )
    row_ids = jnp.arange(poly_block.shape[1], dtype=jnp.int32)
    in_first = row_ids[None, :] < limits[:, None]
    return jnp.where(in_first[:, :, None], product[:, :, 0, :], product[:, :, 1, :])


def shards(fourier, weights, legendre, pair_slots):
    pair_count = pair_slots.shape[0]
    waves = 2 * pair_count
    scaled = fourier * weights[:, None, None]
    seconds = waves - 1 - pair_slots
    slot_order = jnp.stack([pair_slots, seconds], axis=1).reshape(waves)
    packed = jnp.take(scaled, slot_order, axis=1)
    owned = lax.all_to_all(packed, "grid", split_axis=1, concat_axis=0, tiled=True)
    local_pairs = legendre.shape[0]
    own_pairs = lax.dynamic_slice_in_dim(
        pair_slots, lax.axis_index("grid") * local_pairs, local_pairs
    )
    limits = waves - own_pairs
    lat_rows = owned.shape[0]
    lat_block = lax.dynamic_slice_in_dim(legendre, lax.axis_index("layer") * lat_rows, lat_rows, 2)
    partial_value = project(lat_block, owned, limits)
    return lax.psum_scatter(partial_value, "layer", scatter_dimension=2, tiled=True)


def solution(mesh):
    in_specs = (P(("layer", "grid"), None, None), P(("layer", "grid")), P("grid", None, None), P())
    out_specs = P("grid", None, "layer")
    return jax.shard_map(shards, mesh=mesh, in_specs=in_specs, out_specs=out_specs, check_vma=False)
```

profile of v0, /device:TPU:1, one launch (start us, length us, event | category | flops | bytes accessed | tf_op | source)
XLA Modules:
  0.0 183.2 jit_solution(18248349771459491894)
XLA Ops:
  6.5 0.7 broadcast_subtract_fusion
  7.2 0.7 pad_add_fusion
  7.9 0.1 copy.17
  8.0 0.1 reshape.66
  8.2 0.1 reshape.65
  8.4 6.6 %copy_multiply_fusion = f32[8,512,256]{2,0,1:T(8,128)} fusion(f32[8,512,256]{2,1,0:T(8,128)} %param.4, f32[8]{0:T(128)} %param.5), kind=kLoop, calls=%fused_computation.6 | loop fusion | flops 1048576 | bytes 8388640 | tf_op jit(solution)/shard_map/mul | solution.py:25
  14.9 5.1 %gather_fusion = f32[512,8,256]{2,1,0:T(8,128)} fusion(f32[8,512,256]{2,0,1:T(8,128)} %copy_multiply_fusion, s32[1024]{0:T(1024)S(1)} %pad_clamp_fusion), kind=kCustom, calls=%fused_computation | custom fusion | bytes 8390656 | tf_op jit(solution)/shard_map/jit(_take)/gather | solution.py:28
  20.0 4.6 %select_bitcast_fusion = f32[8,512,256]{2,0,1:T(8,128)} fusion(f32[512,8,256]{2,1,0:T(8,128)} %gather_fusion, pred[512]{0:T(512)(128)(4,1)S(1)} %compare_and_fusion), kind=kLoop, calls=%fused_computation.7 | loop fusion | flops 1048576 | bytes 8389120 | tf_op jit(solution)/shard_map/jit(_take)/select_n | solution.py:28
  24.6 0.0 copy-start.1
  24.6 9.5 %all-to-all-start = ((f32[8,512,256]{2,0,1:T(8,128)}), f32[8,512,256]{2,0,1:T(8,128)}, u32[]{:S(2)}, u32[]{:S(2)}) async-start(f32[8,512,256]{2,0,1:T(8,128)} %select_bitcast_fusion), calls=%async_computation | async-start | bytes 8388608 | tf_op jit(solution)/shard_map/all_to_all | solution.py:29
  34.1 0.2 reduce-scatter.2.cloned.1.call-start
  34.3 0.0 copy-done.1
  34.3 0.1 dynamic-slice_subtract_fusion
  34.4 4.4 %constant_dynamic-slice_fusion = f32[8,513,256]{2,0,1:T(8,128)} fusion(f32[8,513,1024]{2,0,1:T(8,128)} %param.6, s32[]{:T(128)S(6)} %select_n.31), kind=kLoop, calls=%fused_computation.16 | loop fusion | bytes 8404996 | tf_op jit(solution)/shard_map/dynamic_slice | solution.py:36
  38.8 0.1 iota_compare_fusion
  38.9 54.4 %all-to-all-done = f32[8,512,256]{2,0,1:T(8,128)} async-done(((f32[8,512,256]{2,0,1:T(8,128)}), f32[8,512,256]{2,0,1:T(8,128)}, u32[]{:S(2)}, u32[]{:S(2)}) %all-to-all-start) | async-done | bytes 4194336 | tf_op jit(solution)/shard_map/all_to_all | solution.py:29
  93.3 0.0 copy-start
  93.3 2.7 %copy.20 = f32[8,32,16,256]{3,0,1,2:T(8,128)S(1)} copy(f32[8,32,16,256]{3,0,2,1:T(8,128)} %bitcast.6) | data formatting | bytes 8388608 | tf_op jit(solution)/shard_map/all_to_all | solution.py:29
  96.0 0.7 copy-done
  96.7 9.0 %fusion.1 = f32[8,513,2,256]{3,1,2,0:T(8,128)S(1)} fusion(f32[256,8,2,256]{3,0,2,1:T(8,128)S(1)} %bitcast.25, f32[8,513,256]{2,0,1:T(8,128)S(1)} %copy-done), kind=kOutput, calls=%fused_computation.5 | convolution fusion | flops 6455033856 | bytes 16801792 | tf_op jit(solution)/shard_map/qrl,lqsc->qrsc/dot_general | solution.py:10
  105.7 2.8 %fusion = f32[8,513,256]{2,1,0:T(8,128)} fusion(f32[8,513,2,256]{3,1,2,0:T(8,128)S(1)} %fusion.1, pred[8,513]{1,0:T(8,128)(4,1)S(1)} %iota_compare_fusion), kind=kLoop, calls=%fused_computation.2 | loop fusion | flops 1050624 | bytes 12611592 | tf_op jit(solution)/shard_map/jit(_where)/select_n | solution.py:19
  108.5 6.4 %copy.22 = f32[8,513,256]{1,0,2:T(8,128)} copy(f32[8,513,256]{2,1,0:T(8,128)} %fusion) | data formatting | bytes 8404992 | tf_op jit(solution)/shard_map/jit(_where)/select_n | solution.py:19
  114.9 0.0 reduce-scatter.2.cloned.1.call-update
  115.0 58.8 %reduce-scatter.2.cloned.1.call-done = f32[8,513,64]{1,0,2:T(8,128)} async-done(((f32[8,513,256]{1,0,2:T(8,128)}), f32[8,513,64]{1,0,2:T(8,128)}) %reduce-scatter.2.cloned.1.call-update) | async-done | bytes 1050640 | tf_op jit(solution)/shard_map/reduce_scatter | solution.py:38
  173.8 2.6 %copy.23 = f32[8,513,64]{1,2,0:T(8,128)} copy(f32[8,513,64]{1,0,2:T(8,128)} %reduce-scatter.2.cloned.1.call-done) | data formatting | bytes 2101248 | tf_op jit(solution)/shard_map/reduce_scatter | solution.py:38
  (3 shorter events, 0.0 us)
Async XLA Ops:
  24.6 9.7 %copy-start.1 = (s32[256]{0:T(256)S(1)}, s32[256]{0:T(256)}, u32[]{:S(2)}) copy-start(s32[256]{0:T(256)} %param.7) | copy-start | bytes 3076
  24.6 68.7 %all-to-all-start = ((f32[8,512,256]{2,0,1:T(8,128)}), f32[8,512,256]{2,0,1:T(8,128)}, u32[]{:S(2)}, u32[]{:S(2)}) async-start(f32[8,512,256]{2,0,1:T(8,128)} %select_bitcast_fusion), calls=%async_computation | async-start | bytes 8388608 | tf_op jit(solution)/shard_map/all_to_all | solution.py:29
  34.1 139.7 %reduce-scatter.2.cloned.1.call-start = ((), (), s32[]{:S(2)}) async-start(), calls=%async_computation.2 | async-start | bytes 6553600 | tf_op jit(solution)/shard_map/reduce_scatter | solution.py:38
  93.3 3.5 %copy-start = (f32[8,513,256]{2,0,1:T(8,128)S(1)}, f32[8,513,256]{2,0,1:T(8,128)}, u32[]{:S(2)}) copy-start(f32[8,513,256]{2,0,1:T(8,128)} %constant_dynamic-slice_fusion) | copy-start | bytes 12607492
Sparse Core Ops, SparseCore 0:
  115.1 58.6 reduce-scatter.1
where the time goes:
time: 184 us; the launch traced here: 183 us
  waiting for transfers between devices  113 us (61%)
  local copies, waits for them, and re-layouts  22.4 us (12%)
  other arithmetic  15.5 us (8%)
  between operations  13.5 us (7%)
  starting transfers between devices  9.69 us (5%)
  matrix products  8.98 us (5%)
    reduce_scatter x1, waiting for transfers between devices, shards(): lax.psum_scatter(partial_value, 'layer', scatter_dimension=2, tiled=True)  58.8 us
    all_to_all x1, waiting for transfers between devices, shards(): lax.all_to_all(packed, 'grid', split_axis=1, concat_axis=0, tiled=True)  54.4 us
    all_to_all x1, starting transfers between devices, shards(): lax.all_to_all(packed, 'grid', split_axis=1, concat_axis=0, tiled=True)  9.47 us
    dot_general x1, matrix products, project(): jnp.einsum('qrl,lqsc->qrsc', poly_block, slots_view, precision=lax.Precis...  8.98 us
    mul x1, other arithmetic, shards(): scaled = fourier * weights[:, None, None]  6.56 us
    select_n x1, local copies, waits for them, and re-layouts, project(): jnp.where(in_first[:, :, None], product[:, :, 0, :], product[:, :, 1, :])  6.41 us
    gather x1, local copies, waits for them, and re-layouts, shards(): packed = jnp.take(scaled, slot_order, axis=1)  5.11 us
    select_n x2, other arithmetic, shards(): packed = jnp.take(scaled, slot_order, axis=1)  4.56 us
  transfers between devices with their start and end apart: 2, of which 2 were waited for; matrix products, arithmetic and copies ran while one was open for 2% of the time, Pallas kernels for 0%

commit v1 on v0

v1 whole, which is shorter than its diff:
```python
import functools

import jax
import jax.numpy as jnp
import numpy as np
from jax import lax
from jax.experimental import pallas as pl
from jax.experimental.pallas import tpu as pltpu
from jax.sharding import Mesh, PartitionSpec as P

AXES = ("zh", "core", "y", "x", "zl")
SIZES = (2, 2, 4, 4, 2)
LAYER = ("zh", "core")
GRID = ("y", "x", "zl")
ORDER = ("zh", "zl", "x", "y", "core")

LATS = 8
PAIRS = 8
LANES = 128
HALF = 64
PITCH = 520
ROWS = 528
VMEM = 60 * 2**20
STEP = 176


def exchange_places():
    ids = np.arange(np.prod(SIZES)).reshape(SIZES)
    order = ids.transpose([AXES.index(a) for a in ORDER]).reshape(-1)
    place = np.empty_like(order)
    place[order] = np.arange(order.size)
    return place


PLACE = exchange_places()


def pack_kernel(slots, weights, fourier, out, rows, blocks, sems, sent):
    waves = fourier.shape[1]

    def fetch(half, lat):
        return pltpu.make_async_copy(
            fourier.at[lat, :, pl.ds(half * LANES, LANES)],
            rows.at[half, pl.ds(lat * PITCH, waves), :],
            sems.at[half, lat],
        )

    for half in range(2):
        for lat in range(LATS):
            fetch(half, lat).start()
    lat_ids = lax.broadcasted_iota(jnp.int32, (LATS, LANES), 0)
    scale = jnp.zeros((LATS, LANES), jnp.float32)
    for lat in range(LATS):
        scale = jnp.where(lat_ids == lat, weights[lat], scale)
    low = lax.broadcasted_iota(jnp.int32, (LATS, LANES), 1) < HALF
    for half in range(2):
        for lat in range(LATS):
            fetch(half, lat).wait()

        @pl.loop(0, 32)
        def _(i):
            zl, x, y = i // 16, (i // 4) % 4, i % 4
            g = (y * 4 + x) * 2 + zl
            place = (half * 32 + i) * 2
            for q in range(PAIRS):
                first = slots[g * PAIRS + q]
                second = waves - 1 - first
                a = rows[half, pl.ds(first, LATS, stride=PITCH), :] * scale
                b = rows[half, pl.ds(second, LATS, stride=PITCH), :] * scale
                turned = pltpu.roll(b, HALF, 1)
                blocks[place, q] = jnp.where(low, a, turned)
                blocks[place + 1, q] = jnp.where(low, turned, a)
            pltpu.make_async_copy(blocks.at[pl.ds(place, 2)], out.at[pl.ds(place, 2)], sent).start()

    pltpu.make_async_copy(blocks, out, sent).wait()


def pack(pair_slots, weights, fourier):
    devices = int(np.prod(SIZES))
    return pl.pallas_call(
        pack_kernel,
        name="pack",
        out_shape=jax.ShapeDtypeStruct((devices, PAIRS, LATS, LANES), jnp.float32),
        in_specs=[
            pl.BlockSpec(memory_space=pltpu.SMEM),
            pl.BlockSpec(memory_space=pltpu.SMEM),
            pl.BlockSpec(memory_space=pl.ANY),
        ],
        out_specs=pl.BlockSpec(memory_space=pl.ANY),
        scratch_shapes=[
            pltpu.VMEM((2, LATS * PITCH, LANES), jnp.float32),
            pltpu.VMEM((devices, PAIRS, LATS, LANES), jnp.float32),
            pltpu.SemaphoreType.DMA((2, LATS)),
            pltpu.SemaphoreType.DMA,
        ],
        compiler_params=pltpu.CompilerParams(vmem_limit_bytes=VMEM),
        cost_estimate=pl.CostEstimate(flops=4 * 2**20, bytes_accessed=8 * 2**20, transcendentals=0),
    )(pair_slots, weights, fourier)


def split_kernel(legendre, high, low):
    rows = legendre.shape[0] // PAIRS
    for q in range(PAIRS):
        part = legendre[pl.ds(q, rows, stride=PAIRS), :]
        top = part.astype(jnp.bfloat16)
        high[q] = top
        low[q] = (part - top.astype(jnp.float32)).astype(jnp.bfloat16)


def split(legendre):
    lats = legendre.shape[1]
    shape = jax.ShapeDtypeStruct((PAIRS, ROWS, lats), jnp.bfloat16)
    spec = pl.BlockSpec((PAIRS, STEP, LANES), lambda i, j: (0, i, j))
    return pl.pallas_call(
        split_kernel,
        name="split",
        grid=(ROWS // STEP, lats // LANES),
        out_shape=(shape, shape),
        in_specs=[pl.BlockSpec((STEP * PAIRS, LANES), lambda i, j: (i, j))],
        out_specs=(spec, spec),
        compiler_params=pltpu.CompilerParams(vmem_limit_bytes=VMEM),
        cost_estimate=pl.CostEstimate(flops=2 * 10**10, bytes_accessed=32 * 2**20, transcendentals=0),
    )(legendre)


def sum_kernel(slots, where, high, low, values, out, terms):
    degrees = out.shape[2]
    q = pl.program_id(0)
    for d in range(0, len(PLACE), 2):
        value = jnp.concatenate([values[int(PLACE[d]), 0], values[int(PLACE[d + 1]), 0]], axis=0)
        top = value.astype(jnp.bfloat16)
        terms[d * LATS : (d + 2) * LATS, :LANES] = top
        terms[d * LATS : (d + 2) * LATS, LANES:] = (value - top.astype(jnp.float32)).astype(jnp.bfloat16)
    dot = functools.partial(jnp.dot, preferred_element_type=jnp.float32)
    wide = dot(high[0], terms[...])
    total = wide[:, :LANES] + wide[:, LANES:] + dot(low[0], terms[:, :LANES])
    turned = total.T[:, :degrees]
    limit = degrees - 1 - slots[where[0] * PAIRS + q]
    in_first = lax.broadcasted_iota(jnp.int32, (HALF, degrees), 1) < limit
    in_low = jnp.logical_xor(in_first, where[1] == 1)
    out[0] = jnp.where(in_low, turned[:HALF], turned[HALF:])


def sums(pair_slots, where, high, low, values, degrees):
    lats = high.shape[2]
    matrix = pl.BlockSpec((1, ROWS, lats), lambda q: (q, 0, 0))
    return pl.pallas_call(
        sum_kernel,
        name="sums",
        grid=(PAIRS,),
        out_shape=jax.ShapeDtypeStruct((PAIRS, HALF, degrees), jnp.float32),
        in_specs=[
            pl.BlockSpec(memory_space=pltpu.SMEM),
            pl.BlockSpec(memory_space=pltpu.SMEM),
            matrix,
            matrix,
            pl.BlockSpec((values.shape[0], 1, LATS, LANES), lambda q: (0, q, 0, 0)),
        ],
        out_specs=pl.BlockSpec((1, HALF, degrees), lambda q: (q, 0, 0)),
        scratch_shapes=[pltpu.VMEM((lats, 2 * LANES), jnp.bfloat16)],
        compiler_params=pltpu.CompilerParams(vmem_limit_bytes=VMEM),
        cost_estimate=pl.CostEstimate(flops=6 * 2**30, bytes_accessed=24 * 2**20, transcendentals=0),
    )(pair_slots, where, high, low, values)


def shards(fourier, weights, legendre, pair_slots):
    degrees, lats = legendre.shape[1:]
    packed = pack(pair_slots, weights, fourier)
    owned = lax.all_to_all(packed, ORDER, split_axis=0, concat_axis=0, tiled=True)
    high, low = split(jnp.transpose(legendre, (1, 0, 2)).reshape(degrees * PAIRS, lats))
    where = jnp.stack([lax.axis_index(GRID), lax.axis_index("core")]).astype(jnp.int32)
    result = sums(pair_slots, where, high, low, owned, degrees)
    return jnp.transpose(result, (0, 2, 1))


def solution(mesh):
    parts = Mesh(mesh.devices.reshape(SIZES), AXES)
    in_specs = (P(AXES, None, None), P(AXES), P(GRID, None, None), P())
    out_specs = P(GRID, None, LAYER)
    return jax.shard_map(shards, mesh=parts, in_specs=in_specs, out_specs=out_specs, check_vma=False)
```

time: 184 us -> 86.3 us (0.47)
  waiting for transfers between devices: 113 us -> 31.5 us
  Pallas kernels: 0 us -> 41.4 us
  local copies, waits for them, and re-layouts: 22.4 us -> 0 us
  other arithmetic: 15.5 us -> 0.59 us
  between operations: 13.5 us -> 0.03 us
  matrix products: 8.98 us -> 0 us
  starting transfers between devices: 9.69 us -> 12 us
    reduce_scatter x1 -> x0, waiting for transfers between devices: 58.8 us -> none  [shards(): lax.psum_scatter(partial_value, 'layer', scatter_dimension=2, tiled=True)]
    pallas_call x0 -> x3, Pallas kernels: none -> 41.4 us  [the longest x1 20.6 us: split(): pl.pallas_call(split_kernel, name='split', grid=(ROWS // STEP, lats // LA...]
    all_to_all x1, waiting for transfers between devices: 54.4 us -> 31.5 us  [shards(): lax.all_to_all(packed, ORDER, split_axis=0, concat_axis=0, tiled=True)]
    dot_general x1 -> x0, matrix products: 8.98 us -> none  [project(): jnp.einsum('qrl,lqsc->qrsc', poly_block, slots_view, precision=lax.Precis...]
    select_n x3 -> x0, other arithmetic: 7.37 us -> none  [the longest x2 4.56 us: shards(): packed = jnp.take(scaled, slot_order, axis=1)]
    mul x1 -> x0, other arithmetic: 6.56 us -> none  [shards(): scaled = fourier * weights[:, None, None]]
    select_n x1 -> x0, local copies, waits for them, and re-layouts: 6.41 us -> none  [project(): jnp.where(in_first[:, :, None], product[:, :, 0, :], product[:, :, 1, :])]
    gather x1 -> x0, local copies, waits for them, and re-layouts: 5.11 us -> none  [shards(): packed = jnp.take(scaled, slot_order, axis=1)]
  transfers between devices with their start and end apart: 2 -> 1, of which waited for: 2 -> 1; matrix products, arithmetic and copies ran while one was open for 2% -> 1% of each run, Pallas kernels for 0% -> 24%
where the time goes in v1:
time: 86.3 us; the launch traced here: 85.5 us
  Pallas kernels  41.4 us (48%)
  waiting for transfers between devices  31.5 us (37%)
  starting transfers between devices  12 us (14%)
    all_to_all x1, waiting for transfers between devices, shards(): lax.all_to_all(packed, ORDER, split_axis=0, concat_axis=0, tiled=True)  31.5 us
    pallas_call x1, Pallas kernels, split(): pl.pallas_call(split_kernel, name='split', grid=(ROWS // STEP, lats // LA...  20.6 us
    pallas_call x1, Pallas kernels, sums(): pl.pallas_call(sum_kernel, name='sums', grid=(PAIRS,), out_shape=jax.Shap...  12.7 us
    all_to_all x1, starting transfers between devices, shards(): lax.all_to_all(packed, ORDER, split_axis=0, concat_axis=0, tiled=True)  12 us
    pallas_call x1, Pallas kernels, pack(): pl.pallas_call(pack_kernel, name='pack', out_shape=jax.ShapeDtypeStruct((...  8.08 us
  transfers between devices with their start and end apart: 1, of which 1 were waited for; matrix products, arithmetic and copies ran while one was open for 1% of the time, Pallas kernels for 24%

profile of v1, /device:TPU:1, one launch (start us, length us, event | category | flops | bytes accessed | tf_op | source)
XLA Modules:
  0.0 85.5 jit_solution(16725363117382875562)
XLA Ops:
  0.0 8.1 %pack.1 = f32[128,8,8,128]{3,2,1,0:T(8,128)} custom-call(s32[256]{0:T(256)} %slots.3, f32[8]{0:T(128)} %weights.1, f32[8,512,256]{2,1,0:T(8,128)} %fourier.1), custom_call_target="tpu_custom_call" | custom-call | flops 4194304 | bytes 8388608 | tf_op jit(solution)/shard_map/pack/pallas_call | solution.py:80
  8.1 12.0 %all-to-all-start = ((f32[128,8,8,128]{3,2,1,0:T(8,128)}), f32[128,8,8,128]{3,2,1,0:T(8,128)}, u32[]{:S(2)}, u32[]{:S(2)}) async-start(f32[128,8,8,128]{3,2,1,0:T(8,128)} %pack.1), calls=%async_computation | async-start | bytes 8388608 | tf_op jit(solution)/shard_map/all_to_all | solution.py:169
  20.1 0.6 pad_add_fusion.where
  20.6 20.6 %split.1 = (bf16[8,528,1024]{2,1,0:T(8,128)(2,1)}, bf16[8,528,1024]{2,1,0:T(8,128)(2,1)}) custom-call(f32[4104,1024]{1,0:T(8,128)} %bitcast.6), custom_call_target="tpu_custom_call" | custom-call | flops 20000000000 | bytes 33554432 | tf_op jit(solution)/shard_map/split/pallas_call | solution.py:114
  41.3 31.5 %all-to-all-done.values = f32[128,8,8,128]{3,2,1,0:T(8,128)} async-done(((f32[128,8,8,128]{3,2,1,0:T(8,128)}), f32[128,8,8,128]{3,2,1,0:T(8,128)}, u32[]{:S(2)}, u32[]{:S(2)}) %all-to-all-start) | async-done | bytes 4194336 | tf_op jit(solution)/shard_map/all_to_all | solution.py:169
  72.8 12.7 %sums.1 = f32[8,64,513]{2,1,0:T(8,128)} custom-call(s32[256]{0:T(256)} %slots.3, s32[2]{0:T(128)} %pad_add_fusion.where, bf16[8,528,1024]{2,1,0:T(8,128)(2,1)} %get-tuple-element.7.high, bf16[8,528,1024]{2,1,0:T(8,128)(2,1)} %get-tuple-element.8.low, f32[128,8,8,128]{3,2,1,0:T(8,128)} %all-to-all-done.values), custom_call_target="tpu_custom_call" | custom-call | flops 6442450944 | bytes 25165824 | tf_op jit(solution)/shard_map/sums/pallas_call | solution.py:147
Async XLA Ops:
  8.1 64.7 %all-to-all-start = ((f32[128,8,8,128]{3,2,1,0:T(8,128)}), f32[128,8,8,128]{3,2,1,0:T(8,128)}, u32[]{:S(2)}, u32[]{:S(2)}) async-start(f32[128,8,8,128]{3,2,1,0:T(8,128)} %pack.1), calls=%async_computation | async-start | bytes 8388608 | tf_op jit(solution)/shard_map/all_to_all | solution.py:169

commit v2 on v1

v2 whole, which is shorter than its diff:
```python
import functools

import jax
import jax.numpy as jnp
import numpy as np
from jax import lax
from jax.experimental import pallas as pl
from jax.experimental.pallas import tpu as pltpu
from jax.sharding import Mesh, PartitionSpec as P

AXES = ("zh", "core", "y", "x", "zl")
SIZES = (2, 2, 4, 4, 2)
LAYER = ("zh", "core")
GRID = ("y", "x", "zl")
ORDER = ("zh", "zl", "x", "y", "core")

LATS = 8
PAIRS = 8
LANES = 128
HALF = 64
PITCH = 520
ROWS = 528
HELD = 3
DEPTH = 3
PARTS = 1
UNROLL = 2
VMEM = 60 * 2**20
STEP = 176


def exchange_places():
    ids = np.arange(np.prod(SIZES)).reshape(SIZES)
    order = ids.transpose([AXES.index(a) for a in ORDER]).reshape(-1)
    place = np.empty_like(order)
    place[order] = np.arange(order.size)
    return place


PLACE = exchange_places()


def pack_kernel(part, slots_in, weights_in, fourier, out, slots, weights, rows, blocks, sems, sent, small):
    waves = fourier.shape[1]
    pairs = blocks.shape[1]
    tables = (
        pltpu.make_async_copy(slots_in, slots, small.at[0]),
        pltpu.make_async_copy(weights_in, weights, small.at[1]),
    )
    for copy in tables:
        copy.start()

    def fetch(half, lat):
        return pltpu.make_async_copy(
            fourier.at[lat, :, pl.ds(half * LANES, LANES)],
            rows.at[half, pl.ds(lat * PITCH, waves), :],
            sems.at[half, lat],
        )

    for half in range(2):
        for lat in range(LATS):
            fetch(half, lat).start()
    for copy in tables:
        copy.wait()
    lat_ids = lax.broadcasted_iota(jnp.int32, (LATS, LANES), 0)
    scale = jnp.zeros((LATS, LANES), jnp.float32)
    for lat in range(LATS):
        scale = jnp.where(lat_ids == lat, weights[lat], scale)
    low = lax.broadcasted_iota(jnp.int32, (LATS, LANES), 1) < HALF
    for half in range(2):
        for lat in range(LATS):
            fetch(half, lat).wait()

        @pl.loop(0, 8 // UNROLL)
        def _(turn):
            for u in range(UNROLL):
                step = turn * UNROLL + u
                zl, x = step >> 2, step & 3
                for y in range(4):
                    place = half * 64 + step * 8 + y * 2
                    for q in range(pairs):
                        first = slots[(x * 2 + zl) * PAIRS + (y * 8 * PAIRS + part * pairs + q)]
                        second = waves - 1 - first
                        a = rows[half, pl.ds(first, LATS, stride=PITCH), :] * scale
                        b = rows[half, pl.ds(second, LATS, stride=PITCH), :] * scale
                        turned = pltpu.roll(b, HALF, 1)
                        blocks[place, q] = jnp.where(low, a, turned)
                        blocks[place + 1, q] = jnp.where(low, turned, a)
            at = pl.ds(half * 64 + turn * UNROLL * 8, UNROLL * 8)
            pltpu.make_async_copy(blocks.at[at], out.at[at], sent).start()

    pltpu.make_async_copy(blocks, out, sent).wait()


def pack(part, pair_slots, weights, fourier):
    shape = (int(np.prod(SIZES)), PAIRS // PARTS, LATS, LANES)
    return pl.pallas_call(
        functools.partial(pack_kernel, part),
        name="pack",
        out_shape=jax.ShapeDtypeStruct(shape, jnp.float32),
        in_specs=[pl.BlockSpec(memory_space=pl.ANY)] * 3,
        out_specs=pl.BlockSpec(memory_space=pl.ANY),
        scratch_shapes=[
            pltpu.SMEM(pair_slots.shape, jnp.int32),
            pltpu.SMEM(weights.shape, jnp.float32),
            pltpu.VMEM((2, LATS * PITCH, LANES), jnp.float32),
            pltpu.VMEM(shape, jnp.float32),
            pltpu.SemaphoreType.DMA((2, LATS)),
            pltpu.SemaphoreType.DMA,
            pltpu.SemaphoreType.DMA((2,)),
        ],
        compiler_params=pltpu.CompilerParams(vmem_limit_bytes=VMEM),
        cost_estimate=pl.CostEstimate(flops=4 * 2**20, bytes_accessed=8 * 2**20, transcendentals=0),
    )(pair_slots, weights, fourier)


def split_kernel(legendre, high, low):
    rows = legendre.shape[0] // PAIRS
    for q in range(PAIRS):
        part = legendre[pl.ds(q, rows, stride=PAIRS), :]
        top = part.astype(jnp.bfloat16)
        high[q] = top
        low[q] = (part - top.astype(jnp.float32)).astype(jnp.bfloat16)


def split(legendre):
    lats = legendre.shape[1]
    shape = jax.ShapeDtypeStruct((PAIRS, ROWS, lats), jnp.bfloat16)
    spec = pl.BlockSpec((PAIRS, STEP, LANES), lambda i, j: (0, i, j))
    return pl.pallas_call(
        split_kernel,
        name="split",
        grid=(ROWS // STEP, lats // LANES),
        out_shape=(shape, shape),
        in_specs=[pl.BlockSpec((STEP * PAIRS, LANES), lambda i, j: (i, j))],
        out_specs=(spec, spec),
        compiler_params=pltpu.CompilerParams(vmem_limit_bytes=VMEM),
        cost_estimate=pl.CostEstimate(flops=2 * 10**10, bytes_accessed=32 * 2**20, transcendentals=0),
    )(legendre)


def hold_kernel(high, low, *rest):
    outs, sems = rest[:-1], rest[-1]
    copies = []
    for i, out in enumerate(outs):
        source = (high, low)[i % 2].at[i // 2]
        copies.append(pltpu.make_async_copy(source, out, sems.at[i]))
    for copy in copies:
        copy.start()
    for copy in copies:
        copy.wait()


def hold(high, low):
    shape = pltpu.VMEM(high.shape[1:], high.dtype)
    return pl.pallas_call(
        hold_kernel,
        name="hold",
        out_shape=[shape] * HELD,
        in_specs=[pl.BlockSpec(memory_space=pl.ANY)] * 2,
        out_specs=[pl.BlockSpec(memory_space=pltpu.VMEM)] * HELD,
        scratch_shapes=[pltpu.SemaphoreType.DMA((HELD,))],
        compiler_params=pltpu.CompilerParams(vmem_limit_bytes=20 * 2**20),
        cost_estimate=pl.CostEstimate(flops=2 * 10**9, bytes_accessed=4 * 2**20, transcendentals=0),
    )(high, low)


def sum_kernel(part, slots_in, where_in, high, low, values, *rest):
    held, out, scratch = rest[:HELD], rest[HELD], rest[HELD + 1 :]
    slots, where, highs, lows, inputs, results, terms, sums, sems, sent, small = scratch
    pairs, _, degrees = results.shape
    tables = (
        pltpu.make_async_copy(slots_in, slots, small.at[0]),
        pltpu.make_async_copy(where_in, where, small.at[1]),
    )

    def fetch_values(q):
        return pltpu.make_async_copy(values.at[:, q], inputs.at[q], sems.at[0, q])

    def fetch_matrix(q):
        terms_of = ((high, highs), (low, lows))
        return [
            pltpu.make_async_copy(source.at[part * pairs + q], target.at[q % DEPTH], sems.at[1 + i, q])
            for i, (source, target) in enumerate(terms_of)
            if 2 * q + i >= HELD
        ]

    def matrix(q, low_term):
        at = 2 * q + low_term
        return held[at][...] if at < HELD else (highs, lows)[low_term][q % DEPTH]

    def start(q):
        if q < pairs:
            for copy in fetch_matrix(q):
                copy.start()
        if q + 1 < pairs:
            fetch_values(q + 1).start()

    def prepare(q):
        for d in range(0, len(PLACE), 2):
            value = jnp.concatenate([inputs[q, int(PLACE[d])], inputs[q, int(PLACE[d + 1])]], axis=0)
            top = value.astype(jnp.bfloat16)
            at = pl.ds(d * LATS, 2 * LATS)
            terms[q % 2, at, :LANES] = top
            terms[q % 2, at, LANES:] = (value - top.astype(jnp.float32)).astype(jnp.bfloat16)

    def multiply(q):
        dot = functools.partial(jnp.dot, preferred_element_type=jnp.float32)
        wide = dot(matrix(q, 0), terms[q % 2])
        sums[q % 2] = wide[:, :LANES] + wide[:, LANES:] + dot(matrix(q, 1), terms[q % 2, :, :LANES])

    def finish(q):
        turned = sums[q % 2].T[:, :degrees]
        limit = degrees - 1 - slots[where[0] * PAIRS + part * pairs + q]
        in_first = lax.broadcasted_iota(jnp.int32, (HALF, degrees), 1) < limit
        in_low = jnp.logical_xor(in_first, where[1] == 1)
        results[q] = jnp.where(in_low, turned[:HALF], turned[HALF:])

    def send(q):
        pltpu.make_async_copy(results.at[q], out.at[q], sent).start()

    fetch_values(0).start()
    for q in range(DEPTH - 1):
        start(q)
    for copy in tables:
        copy.start()
    for copy in tables:
        copy.wait()
    fetch_values(0).wait()
    prepare(0)
    for q in range(pairs):
        start(q + DEPTH - 1)
        for copy in fetch_matrix(q):
            copy.wait()
        if q + 1 < pairs:
            fetch_values(q + 1).wait()
            prepare(q + 1)
        multiply(q)
        if q:
            finish(q - 1)
            send(q - 1)
    finish(pairs - 1)
    send(pairs - 1)
    pltpu.make_async_copy(results, out, sent).wait()


def sums(part, pair_slots, where, high, low, values, held, degrees):
    lats = high.shape[2]
    devices, pairs = values.shape[:2]
    any_space = pl.BlockSpec(memory_space=pl.ANY)
    return pl.pallas_call(
        functools.partial(sum_kernel, part),
        name="sums",
        out_shape=jax.ShapeDtypeStruct((pairs, HALF, degrees), jnp.float32),
        in_specs=[any_space] * 5 + [pl.BlockSpec(memory_space=pltpu.VMEM)] * HELD,
        out_specs=any_space,
        scratch_shapes=[
            pltpu.SMEM(pair_slots.shape, jnp.int32),
            pltpu.SMEM(where.shape, jnp.int32),
            pltpu.VMEM((DEPTH, ROWS, lats), jnp.bfloat16),
            pltpu.VMEM((DEPTH, ROWS, lats), jnp.bfloat16),
            pltpu.VMEM((pairs, devices, LATS, LANES), jnp.float32),
            pltpu.VMEM((pairs, HALF, degrees), jnp.float32),
            pltpu.VMEM((2, lats, 2 * LANES), jnp.bfloat16),
            pltpu.VMEM((2, ROWS, LANES), jnp.float32),
            pltpu.SemaphoreType.DMA((3, pairs)),
            pltpu.SemaphoreType.DMA,
            pltpu.SemaphoreType.DMA((2,)),
        ],
        compiler_params=pltpu.CompilerParams(vmem_limit_bytes=40 * 2**20),
        cost_estimate=pl.CostEstimate(flops=6 * 2**30 // PARTS, bytes_accessed=24 * 2**20 // PARTS, transcendentals=0),
    )(pair_slots, where, high, low, values, *held)


def shards(fourier, weights, legendre, pair_slots):
    degrees, lats = legendre.shape[1:]
    owned = []
    for part in range(PARTS):
        packed = pack(part, pair_slots, weights, fourier)
        owned.append(lax.all_to_all(packed, ORDER, split_axis=0, concat_axis=0, tiled=True))
    high, low = split(jnp.transpose(legendre, (1, 0, 2)).reshape(degrees * PAIRS, lats))
    held = hold(high, low)
    where = jnp.stack([lax.axis_index(GRID), lax.axis_index("core")]).astype(jnp.int32)
    results = [sums(part, pair_slots, where, high, low, owned[part], held, degrees) for part in range(PARTS)]
    result = results[0] if PARTS == 1 else jnp.concatenate(results, axis=0)
    return jnp.transpose(result, (0, 2, 1))


def solution(mesh):
    parts = Mesh(mesh.devices.reshape(SIZES), AXES)
    in_specs = (P(AXES, None, None), P(AXES), P(GRID, None, None), P())
    out_specs = P(GRID, None, LAYER)
    return jax.shard_map(shards, mesh=parts, in_specs=in_specs, out_specs=out_specs, check_vma=False)
```

time: 86.3 us -> 78.2 us (0.906)
  Pallas kernels: 41.4 us -> 34 us
  waiting for transfers between devices: 31.5 us -> 24.4 us
  local copies, waits for them, and re-layouts: 0 us -> 6.92 us
    pallas_call x2 -> x3, Pallas kernels: 20.8 us -> 13.1 us  [the longest x1 8.85 us: sums(): pl.pallas_call(functools.partial(sum_kernel, part), name='sums', out_shap...]
    all_to_all x1, waiting for transfers between devices: 31.5 us -> 24.4 us  [shards(): lax.all_to_all(packed, ORDER, split_axis=0, concat_axis=0, tiled=True)]
    unnamed x0 -> x6, local copies, waits for them, and re-layouts: none -> 6.92 us
  transfers between devices with their start and end apart: 1 -> 1, of which waited for: 1 -> 1; matrix products, arithmetic and copies ran while one was open for 1% -> 0% of each run, Pallas kernels for 24% -> 28%
where the time goes in v2:
time: 78.2 us; the launch traced here: 77.4 us
  Pallas kernels  34 us (43%)
  waiting for transfers between devices  24.4 us (31%)
  starting transfers between devices  12 us (15%)
  local copies, waits for them, and re-layouts  6.92 us (9%)
    all_to_all x1, waiting for transfers between devices, shards(): lax.all_to_all(packed, ORDER, split_axis=0, concat_axis=0, tiled=True)  24.4 us
    pallas_call x1, Pallas kernels, split(): pl.pallas_call(split_kernel, name='split', grid=(ROWS // STEP, lats // LA...  20.9 us
    all_to_all x1, starting transfers between devices, shards(): lax.all_to_all(packed, ORDER, split_axis=0, concat_axis=0, tiled=True)  12 us
    pallas_call x1, Pallas kernels, sums(): pl.pallas_call(functools.partial(sum_kernel, part), name='sums', out_shap...  8.85 us
    unnamed x6, local copies, waits for them, and re-layouts  6.92 us
    pallas_call x1, Pallas kernels, pack(): pl.pallas_call(functools.partial(pack_kernel, part), name='pack', out_sha...  3.87 us
  transfers between devices with their start and end apart: 1, of which 1 were waited for; matrix products, arithmetic and copies ran while one was open for 0% of the time, Pallas kernels for 28%

profile of v2, /device:TPU:1, one launch (start us, length us, event | category | flops | bytes accessed | tf_op | source)
XLA Modules:
  0.0 77.4 jit_solution(8641051694215483731)
XLA Ops:
  0.0 3.9 %pack.1 = f32[128,8,8,128]{3,2,1,0:T(8,128)} custom-call(s32[256]{0:T(256)} %slots_in.3, f32[8]{0:T(128)} %weights_in.1, f32[8,512,256]{2,1,0:T(8,128)} %fourier.1), custom_call_target="tpu_custom_call" | custom-call | flops 4194304 | bytes 8388608 | tf_op jit(solution)/shard_map/pack/pallas_call | solution.py:96
  3.9 12.0 %all-to-all-start = ((f32[128,8,8,128]{3,2,1,0:T(8,128)}), f32[128,8,8,128]{3,2,1,0:T(8,128)}, u32[]{:S(2)}, u32[]{:S(2)}) async-start(f32[128,8,8,128]{3,2,1,0:T(8,128)} %pack.1), calls=%async_computation | async-start | bytes 8388608 | tf_op jit(solution)/shard_map/all_to_all | solution.py:279
  15.8 0.1 pad_add_fusion.where_in
  15.9 20.9 %split.1 = (bf16[8,528,1024]{2,1,0:T(8,128)(2,1)}, bf16[8,528,1024]{2,1,0:T(8,128)(2,1)}) custom-call(f32[4104,1024]{1,0:T(8,128)} %bitcast.6), custom_call_target="tpu_custom_call" | custom-call | flops 20000000000 | bytes 33554432 | tf_op jit(solution)/shard_map/split/pallas_call | solution.py:129
  36.9 0.0 copy-start
  36.9 3.5 %copy-done = bf16[8,528,1024]{2,1,0:T(8,128)(2,1)S(1)} copy-done((bf16[8,528,1024]{2,1,0:T(8,128)(2,1)S(1)}, bf16[8,528,1024]{2,1,0:T(8,128)(2,1)}, u32[]{:S(2)}) %copy-start) | copy-done | bytes 8650776
  40.3 0.0 copy-start.1
  40.3 3.5 %copy-done.1 = bf16[8,528,1024]{2,1,0:T(8,128)(2,1)S(1)} copy-done((bf16[8,528,1024]{2,1,0:T(8,128)(2,1)S(1)}, bf16[8,528,1024]{2,1,0:T(8,128)(2,1)}, u32[]{:S(2)}) %copy-start.1) | copy-done | bytes 8650776
  43.8 0.0 copy-start.2
  43.8 0.4 hold.1
  44.1 24.4 %all-to-all-done.values = f32[128,8,8,128]{3,2,1,0:T(8,128)} async-done(((f32[128,8,8,128]{3,2,1,0:T(8,128)}), f32[128,8,8,128]{3,2,1,0:T(8,128)}, u32[]{:S(2)}, u32[]{:S(2)}) %all-to-all-start) | async-done | bytes 4194336 | tf_op jit(solution)/shard_map/all_to_all | solution.py:279
  68.6 0.0 copy-done.2
  68.6 8.8 %sums.1 = f32[8,64,513]{2,1,0:T(8,128)} custom-call(s32[256]{0:T(256)S(1)} %copy-done.2, s32[2]{0:T(128)S(1)} %pad_add_fusion.where_in, bf16[8,528,1024]{2,1,0:T(8,128)(2,1)} %get-tuple-element.10.high, bf16[8,528,1024]{2,1,0:T(8,128)(2,1)} %get-tuple-element.11.low, f32[128,8,8,128]{3,2,1,0:T(8,128)} %all-to-all-done.values, ...), custom_call_target="tpu_custom_call" | custom-call | flops 6442450944 | bytes 25165824 | tf_op jit(solution)/shard_map/sums/pallas_call | solution.py:250
Async XLA Ops:
  3.9 64.7 %all-to-all-start = ((f32[128,8,8,128]{3,2,1,0:T(8,128)}), f32[128,8,8,128]{3,2,1,0:T(8,128)}, u32[]{:S(2)}, u32[]{:S(2)}) async-start(f32[128,8,8,128]{3,2,1,0:T(8,128)} %pack.1), calls=%async_computation | async-start | bytes 8388608 | tf_op jit(solution)/shard_map/all_to_all | solution.py:279
  36.9 3.5 %copy-start = (bf16[8,528,1024]{2,1,0:T(8,128)(2,1)S(1)}, bf16[8,528,1024]{2,1,0:T(8,128)(2,1)}, u32[]{:S(2)}) copy-start(bf16[8,528,1024]{2,1,0:T(8,128)(2,1)} %get-tuple-element.10.high) | copy-start | bytes 25952260
  40.3 3.5 %copy-start.1 = (bf16[8,528,1024]{2,1,0:T(8,128)(2,1)S(1)}, bf16[8,528,1024]{2,1,0:T(8,128)(2,1)}, u32[]{:S(2)}) copy-start(bf16[8,528,1024]{2,1,0:T(8,128)(2,1)} %get-tuple-element.11.low) | copy-start | bytes 25952260
  43.8 24.8 %copy-start.2 = (s32[256]{0:T(256)S(1)}, s32[256]{0:T(256)}, u32[]{:S(2)}) copy-start(s32[256]{0:T(256)} %slots_in.3) | copy-start | bytes 3076
